TPU v7x, 32 devices: a whole 2x2x4 slice. The times are simulated.
32 devices in a mesh: gx: 32 (over z, y, x, core).
Axes of the slice: x: 2, y: 2, z: 4, core: 2. Of those that a mesh axis runs over, the one named last changes fastest.
Arguments:
- populations0: float32 [27, 32, 2048], P(None, 'gx'), as said below
- force: float32 [3, 32, 2048], P(None, 'gx'), may hold values from -0.05 to 0.05
- solid: int32 [32, 2048], P('gx'), may hold values 0 or 1
- newton_count: int32 [32, 2048], P('gx'), may hold values from 1 to 3
- cotangent: float32 [27, 32, 2048], P(None, 'gx'), may hold values from -6 to 6
Outputs:
- final_ratio: float32 [27, 32, 2048], P(None, 'gx')
- grad_populations: float32 [27, 32, 2048], P(None, 'gx')
- grad_force: float32 [3, 32, 2048], P(None, 'gx')
Inputs may be any that keep to these rules, and one draw needn't show every extreme that they name: `populations0`: every population lies between 0.6 and 1.4 times its lattice weight.
All inputs are finite; a program needn't handle non-finite values. No bound on the sum of `solid` on one device may be relied on, other than what follows from the above.
Results may differ from a plain program's by a relative error of at most 0.0003.
Values sent between devices are 32-bit elements; how exact they have to be, the bound alone decides.
No kernel may reach another device: no remote copies, remote signals or barrier semaphores. Data moves between devices by JAX's collectives and lax.ppermute only.
A program may use at most 64 MiB of HBM per device.

v0:
```python
import jax
import jax.numpy as jnp
import numpy as np
from jax import lax
from jax.sharding import PartitionSpec as P

NY = 16
NZ = 128
STEPS = 4
NEWTON = 3


BETA = 0.85


def passed_along(x, axis, by):
    devices = lax.axis_size(axis)
    return lax.ppermute(x, axis, [(i, (i + by) % devices) for i in range(devices)])


def tables():
    speeds_table = np.array([[a, b, c] for a in (-1, 0, 1) for b in (-1, 0, 1) for c in (-1, 0, 1)])
    levels = np.abs(speeds_table).sum(axis=1)
    weight_table = np.array([8.0 / 27.0, 2.0 / 27.0, 1.0 / 54.0, 1.0 / 216.0])[levels]
    return (speeds_table, weight_table)


def collide(populations, force, solid, newton_count):
    speeds_table, weight_table = tables()
    velocity = jnp.asarray(speeds_table, jnp.float32)
    weight = jnp.asarray(weight_table, jnp.float32)[:, None, None]
    density = jnp.sum(populations, axis=0)
    momentum = jnp.einsum("iq,ixs->qxs", velocity, populations, precision=lax.Precision.HIGHEST)
    bulk_velocity = (momentum + force) / density
    projected = jnp.einsum("iq,qxs->ixs", velocity, bulk_velocity, precision=lax.Precision.HIGHEST)
    squared_speed = jnp.sum(bulk_velocity * bulk_velocity, axis=0)
    balance = (
        weight
        * density
        * (1.0 + 3.0 * projected + 4.5 * projected * projected - 1.5 * squared_speed)
    )
    offset = balance - populations
    entropy = jnp.sum(populations * jnp.log(populations / weight), axis=0)
    reaches = jnp.where(
        offset < 0.0, populations / jnp.maximum(-offset, 0.001 * weight), 1000000000.0
    )
    ceiling = jnp.clip(0.9 * jnp.min(reaches, axis=0), 1.0, 2.0)
    factor = ceiling
    for iteration in range(NEWTON):
        blended = populations + factor * offset
        logged = jnp.log(blended / weight)
        excess = jnp.sum(blended * logged, axis=0) - entropy
        derivative = jnp.sum(offset * (logged + 1.0), axis=0)
        bending = jnp.sum(offset * offset / blended, axis=0)
        update = jnp.clip(factor - excess / jnp.maximum(derivative, 0.5 * bending), 1.0, ceiling)
        factor = jnp.where(newton_count > iteration, update, factor)
    factor = lax.stop_gradient(factor)
    relaxed = populations + BETA * factor * offset
    return jnp.where(solid[None] == 1, populations[::-1], relaxed)


def plane_rolls(values, sign):
    planes = values.shape[1]
    lattice = values.reshape(27, planes, NY, NZ)
    groups = []
    for along_y in (-1, 0, 1):
        for along_z in (-1, 0, 1):
            member = lattice[(along_y + 1) * 3 + (along_z + 1) :: 9]
            groups.append(jnp.roll(member, (sign * along_y, sign * along_z), axis=(2, 3)))
    return jnp.stack(groups, axis=1).reshape(27, planes, NY * NZ)


def cross_forward(post):
    planes = post.shape[1]
    from_left = passed_along(post[18:27, planes - 1 : planes], "gx", 1)
    from_right = passed_along(post[0:9, 0:1], "gx", -1)
    lower = jnp.concatenate([post[0:9, 1:], from_right], axis=1)
    upper = jnp.concatenate([from_left, post[18:27, : planes - 1]], axis=1)
    return jnp.concatenate([lower, post[9:18], upper], axis=0)


def cross_backward(adjoint):
    planes = adjoint.shape[1]
    from_right = passed_along(adjoint[18:27, 0:1], "gx", -1)
    from_left = passed_along(adjoint[0:9, planes - 1 : planes], "gx", 1)
    upper = jnp.concatenate([adjoint[18:27, 1:], from_right], axis=1)
    lower = jnp.concatenate([from_left, adjoint[0:9, : planes - 1]], axis=1)
    return jnp.concatenate([lower, adjoint[9:18], upper], axis=0)


def on_device(populations0, force, solid, newton_count, cotangent):

    def local_collide(values, pushed):
        return collide(values, pushed, solid, newton_count)

    stored = []
    state = populations0
    for section in range(STEPS):
        stored.append(state)
        state = plane_rolls(cross_forward(local_collide(state, force)), 1)
    adjoint = cotangent
    grad_push = jnp.zeros_like(force)
    for section in reversed(range(STEPS)):
        through = cross_backward(plane_rolls(adjoint, -1))
        unused, pullback = jax.vjp(local_collide, stored[section], force)
        adjoint, term = pullback(through)
        grad_push = grad_push + term
    speeds_table, weight_table = tables()
    weight = jnp.asarray(weight_table, jnp.float32)[:, None, None]
    return (state / weight, adjoint, grad_push)


def solution(mesh):
    return jax.shard_map(
        on_device,
        mesh=mesh,
        in_specs=(
            P(None, "gx", None),
            P(None, "gx", None),
            P("gx", None),
            P("gx", None),
            P(None, "gx", None),
        ),
        out_specs=(P(None, "gx", None), P(None, "gx", None), P(None, "gx", None)),
        check_vma=False,
    )
```

profile of v0, /device:TPU:0, one launch (start us, length us, event | category | flops | bytes accessed | tf_op | source)
XLA Modules:
  0.0 94.1 jit_solution(13921353206531315713)
XLA Ops:
  0.7 1.1 %reduce_sum.1378 = f32[2048]{0:T(1024)S(1)} reduce(f32[27,1,2048]{2,1,0:T(1,128)} %param.22, f32[]{:T(128)} %constant.20.clone.1), dimensions={0,1}, to_apply=%region_0.0 | reduce | flops 53248 | bytes 229380 | tf_op jit(solution)/shard_map/reduce_sum | solution.py:32
  1.8 1.1 %multiply_reduce_fusion.15 = (f32[2048]{0:T(1024)S(1)}, f32[3,1,2048]{2,0,1:T(4,128)S(1)}) fusion(f32[2048]{0:T(1024)S(1)} %reduce_sum.1378, f32[3,1,2048]{2,1,0:T(1,128)} %param.23, f32[27,3]{1,0:T(8,128)S(1)} %copy-done.2, f32[27,1,2048]{2,1,0:T(1,128)S(1)} %copy-done), kind=kOutput, calls=%fused_computation.335 | convolution fusion | flops 2013184 | bytes 287044 | tf_op jit(solution)/shard_map/iq,ixs->qxs/dot_general | solution.py:33
  2.9 0.6 copy-done.4
  3.6 0.5 select_reduce_fusion.3
  4.1 0.6 copy-done.6
  4.8 0.4 fusion.97
  5.2 0.7 copy-done.1
  5.8 0.3 fusion.90
  6.2 0.3 fusion.85
  6.6 0.4 rev.24
  7.0 0.2 copy-done.8
  7.5 6.5 %collective-permute-start = (f32[9,1,2048]{2,0,1:T(8,128)S(1)}, f32[9,1,2048]{2,0,1:T(8,128)S(1)}, u32[]{:S(2)}, u32[]{:S(2)}) collective-permute-start(f32[9,1,2048]{2,0,1:T(8,128)S(1)} %get-tuple-element.79), channel_id=1, source_target_pairs={{0,31},{1,0},{2,1},{3,2},{4,3},{5,4},{6,5},{7,6},{8,7},{9,8},{10,9... | collective-permute-start | bytes 221192 | tf_op jit(solution)/shard_map/ppermute | solution.py:18
  15.1 1.4 %collective-permute-done = f32[9,1,2048]{2,0,1:T(8,128)S(1)} collective-permute-done((f32[9,1,2048]{2,0,1:T(8,128)S(1)}, f32[9,1,2048]{2,0,1:T(8,128)S(1)}, u32[]{:S(2)}, u32[]{:S(2)}) %collective-permute-start) | collective-permute-done | bytes 73760 | tf_op jit(solution)/shard_map/ppermute | solution.py:18
  16.5 5.5 %collective-permute-done.1 = f32[9,1,2048]{2,0,1:T(8,128)S(1)} collective-permute-done((f32[9,1,2048]{2,0,1:T(8,128)S(1)}, f32[9,1,2048]{2,0,1:T(8,128)S(1)}, u32[]{:S(2)}, u32[]{:S(2)}) %collective-permute-start.1) | collective-permute-done | bytes 73760 | tf_op jit(solution)/shard_map/ppermute | solution.py:18
  23.8 0.7 copy-done.3
  24.5 0.3 multiply_reduce_fusion.14
  24.8 0.5 select_reduce_fusion.2
  25.3 0.7 copy-done.7
  26.1 0.3 fusion.80
  26.5 0.3 fusion.75
  26.8 0.3 fusion.70
  27.2 0.4 rev.25
  27.9 0.5 collective-permute-start.3
  28.6 5.4 %collective-permute-start.9 = (f32[9,1,2048]{2,0,1:T(8,128)S(1)}, f32[9,1,2048]{2,0,1:T(8,128)S(1)}, u32[]{:S(2)}, u32[]{:S(2)}) collective-permute-start(f32[9,1,2048]{2,0,1:T(8,128)S(1)} %copy.131), channel_id=1, source_target_pairs={{0,31},{1,0},{2,1},{3,2},{4,3},{5,4},{6,5},{7,6},{8,7},{9,8},{10,9... | collective-permute-start | bytes 221192 | tf_op jit(solution)/shard_map/ppermute | solution.py:18
  34.0 2.1 %collective-permute-done.3 = f32[9,1,2048]{2,0,1:T(8,128)S(1)} collective-permute-done((f32[9,1,2048]{2,0,1:T(8,128)S(1)}, f32[9,1,2048]{2,0,1:T(8,128)S(1)}, u32[]{:S(2)}, u32[]{:S(2)}) %collective-permute-start.3) | collective-permute-done | bytes 73760 | tf_op jit(solution)/shard_map/ppermute | solution.py:18
  38.2 0.3 multiply_reduce_fusion.13
  38.5 0.5 select_reduce_fusion.1
  39.0 0.3 fusion.65
  39.3 0.3 fusion.60
  39.7 0.3 fusion.55
  40.1 0.4 rev.26
  40.8 0.5 collective-permute-start.5
  41.4 1.9 %collective-permute-done.4 = f32[9,1,2048]{2,0,1:T(8,128)S(1)} collective-permute-done((f32[9,1,2048]{2,0,1:T(8,128)S(1)}, f32[9,1,2048]{2,0,1:T(8,128)S(1)}, u32[]{:S(2)}, u32[]{:S(2)}) %collective-permute-start.4) | collective-permute-done | bytes 73760 | tf_op jit(solution)/shard_map/ppermute | solution.py:18
  43.3 5.7 %collective-permute-done.5 = f32[9,1,2048]{2,0,1:T(8,128)S(1)} collective-permute-done((f32[9,1,2048]{2,0,1:T(8,128)S(1)}, f32[9,1,2048]{2,0,1:T(8,128)S(1)}, u32[]{:S(2)}, u32[]{:S(2)}) %collective-permute-start.5) | collective-permute-done | bytes 73760 | tf_op jit(solution)/shard_map/ppermute | solution.py:18
  51.1 0.3 multiply_reduce_fusion.12
  51.4 0.5 select_reduce_fusion
  51.9 0.3 fusion.50
  52.3 0.3 fusion.45
  52.6 0.3 fusion.40
  53.1 0.4 rev.27
  53.5 0.2 broadcast_select_fusion.3
  54.0 0.5 multiply_reduce_fusion.11
  54.4 0.4 convolution_bitcast_fusion.3
  54.8 0.4 rev.28
  56.8 5.4 %collective-permute-start.11 = (f32[9,1,2048]{2,0,1:T(8,128)S(1)}, f32[9,1,2048]{2,0,1:T(8,128)S(1)}, u32[]{:S(2)}, u32[]{:S(2)}) collective-permute-start(f32[9,1,2048]{2,0,1:T(8,128)S(1)} %copy.142), channel_id=1, source_target_pairs={{0,31},{1,0},{2,1},{3,2},{4,3},{5,4},{6,5},{7,6},{8,7},{9,8},{10,9... | collective-permute-start | bytes 221192 | tf_op jit(solution)/shard_map/ppermute | solution.py:18
  62.3 0.5 collective-permute-start.7
  62.8 1.9 %collective-permute-done.10 = f32[9,1,2048]{2,0,1:T(8,128)S(1)} collective-permute-done((f32[9,1,2048]{2,0,1:T(8,128)S(1)}, f32[9,1,2048]{2,0,1:T(8,128)S(1)}, u32[]{:S(2)}, u32[]{:S(2)}) %collective-permute-start.10) | collective-permute-done | bytes 73760 | tf_op jit(solution)/shard_map/ppermute | solution.py:18
  65.0 0.5 multiply_reduce_fusion.10
  65.5 0.3 convolution_bitcast_fusion.2
  65.8 0.4 rev.29
  66.6 3.8 %collective-permute-done.7 = f32[9,1,2048]{2,0,1:T(8,128)S(1)} collective-permute-done((f32[9,1,2048]{2,0,1:T(8,128)S(1)}, f32[9,1,2048]{2,0,1:T(8,128)S(1)}, u32[]{:S(2)}, u32[]{:S(2)}) %collective-permute-start.7) | collective-permute-done | bytes 73760 | tf_op jit(solution)/shard_map/ppermute | solution.py:18
  71.8 5.4 %collective-permute-start.13 = (f32[9,1,2048]{2,0,1:T(8,128)S(1)}, f32[9,1,2048]{2,0,1:T(8,128)S(1)}, u32[]{:S(2)}, u32[]{:S(2)}) collective-permute-start(f32[9,1,2048]{2,0,1:T(8,128)S(1)} %copy.153), channel_id=1, source_target_pairs={{0,31},{1,0},{2,1},{3,2},{4,3},{5,4},{6,5},{7,6},{8,7},{9,8},{10,9... | collective-permute-start | bytes 221192 | tf_op jit(solution)/shard_map/ppermute | solution.py:18
  78.3 1.4 %collective-permute-done.12 = f32[9,1,2048]{2,0,1:T(8,128)S(1)} collective-permute-done((f32[9,1,2048]{2,0,1:T(8,128)S(1)}, f32[9,1,2048]{2,0,1:T(8,128)S(1)}, u32[]{:S(2)}, u32[]{:S(2)}) %collective-permute-start.12) | collective-permute-done | bytes 73760 | tf_op jit(solution)/shard_map/ppermute | solution.py:18
  80.0 0.5 multiply_reduce_fusion.9
  80.5 0.4 convolution_bitcast_fusion.1
  80.9 0.4 rev.30
  82.8 5.5 %collective-permute-start.15 = (f32[9,1,2048]{2,0,1:T(8,128)S(1)}, f32[9,1,2048]{2,0,1:T(8,128)S(1)}, u32[]{:S(2)}, u32[]{:S(2)}) collective-permute-start(f32[9,1,2048]{2,0,1:T(8,128)S(1)} %copy.164), channel_id=1, source_target_pairs={{0,31},{1,0},{2,1},{3,2},{4,3},{5,4},{6,5},{7,6},{8,7},{9,8},{10,9... | collective-permute-start | bytes 221192 | tf_op jit(solution)/shard_map/ppermute | solution.py:18
  88.4 0.9 copy.166
  89.4 1.4 %collective-permute-done.14 = f32[9,1,2048]{2,0,1:T(8,128)S(1)} collective-permute-done((f32[9,1,2048]{2,0,1:T(8,128)S(1)}, f32[9,1,2048]{2,0,1:T(8,128)S(1)}, u32[]{:S(2)}, u32[]{:S(2)}) %collective-permute-start.14) | collective-permute-done | bytes 73760 | tf_op jit(solution)/shard_map/ppermute | solution.py:18
  91.2 0.5 add_add_fusion.4
  91.6 0.4 convolution_bitcast_fusion
  92.0 0.4 rev.31
  92.6 0.9 copy.167
  93.5 0.6 copy.168
  (380 shorter events, 15.0 us)
Async XLA Ops:
  0.6 1.2 %copy-start.2 = (f32[27,3]{1,0:T(8,128)S(1)}, f32[27,3]{1,0:T(8,128)}, u32[]{:S(2)}) copy-start(f32[27,3]{1,0:T(8,128)} %constant.16.clone) | copy-start | bytes 976
  0.6 1.2 %copy-start = (f32[27,1,2048]{2,1,0:T(1,128)S(1)}, f32[27,1,2048]{2,1,0:T(1,128)}, u32[]{:S(2)}) copy-start(f32[27,1,2048]{2,1,0:T(1,128)} %param.22) | copy-start | bytes 663556
  2.9 0.7 copy-start.4
  2.9 0.7 copy-start.9
  4.1 0.7 copy-start.6
  5.1 0.7 copy-start.1
  6.6 0.7 copy-start.8
  7.5 6.5 %copy-start.5 = (f32[27,1,2048]{2,1,0:T(1,128)S(1)}, f32[27,1,2048]{2,1,0:T(1,128)}, u32[]{:S(2)}) copy-start(f32[27,1,2048]{2,1,0:T(1,128)} %param.26) | copy-start | bytes 663556
  7.5 9.0 %collective-permute-start = (f32[9,1,2048]{2,0,1:T(8,128)S(1)}, f32[9,1,2048]{2,0,1:T(8,128)S(1)}, u32[]{:S(2)}, u32[]{:S(2)}) collective-permute-start(f32[9,1,2048]{2,0,1:T(8,128)S(1)} %get-tuple-element.79), channel_id=1, source_target_pairs={{0,31},{1,0},{2,1},{3,2},{4,3},{5,4},{6,5},{7,6},{8,7},{9,8},{10,9... | collective-permute-start | bytes 221192 | tf_op jit(solution)/shard_map/ppermute | solution.py:18
  14.0 8.0 %collective-permute-start.1 = (f32[9,1,2048]{2,0,1:T(8,128)S(1)}, f32[9,1,2048]{2,0,1:T(8,128)S(1)}, u32[]{:S(2)}, u32[]{:S(2)}) collective-permute-start(f32[9,1,2048]{2,0,1:T(8,128)S(1)} %get-tuple-element.80), channel_id=1, source_target_pairs={{0,1},{1,2},{2,3},{3,4},{4,5},{5,6},{6,7},{7,8},{8,9},{9,10},{10,1... | collective-permute-start | bytes 221192 | tf_op jit(solution)/shard_map/ppermute | solution.py:18
  23.8 0.7 copy-start.3
  25.3 0.7 copy-start.7
  27.9 6.1 %collective-permute-start.2 = (f32[9,1,2048]{2,0,1:T(8,128)S(1)}, f32[9,1,2048]{2,0,1:T(8,128)S(1)}, u32[]{:S(2)}, u32[]{:S(2)}) collective-permute-start(f32[9,1,2048]{2,0,1:T(8,128)S(1)} %get-tuple-element.74), channel_id=1, source_target_pairs={{0,31},{1,0},{2,1},{3,2},{4,3},{5,4},{6,5},{7,6},{8,7},{9,8},{10,9... | collective-permute-start | bytes 221192 | tf_op jit(solution)/shard_map/ppermute | solution.py:18
  27.9 8.1 %collective-permute-start.3 = (f32[9,1,2048]{2,0,1:T(8,128)S(1)}, f32[9,1,2048]{2,0,1:T(8,128)S(1)}, u32[]{:S(2)}, u32[]{:S(2)}) collective-permute-start(f32[9,1,2048]{2,0,1:T(8,128)S(1)} %get-tuple-element.75), channel_id=1, source_target_pairs={{0,1},{1,2},{2,3},{3,4},{4,5},{5,6},{6,7},{7,8},{8,9},{9,10},{10,1... | collective-permute-start | bytes 221192 | tf_op jit(solution)/shard_map/ppermute | solution.py:18
  28.5 25.0 %collective-permute-start.8 = (f32[9,1,2048]{2,0,1:T(8,128)S(1)}, f32[9,1,2048]{2,0,1:T(8,128)S(1)}, u32[]{:S(2)}, u32[]{:S(2)}) collective-permute-start(f32[9,1,2048]{2,0,1:T(8,128)S(1)} %copy.130), channel_id=1, source_target_pairs={{0,1},{1,2},{2,3},{3,4},{4,5},{5,6},{6,7},{7,8},{8,9},{9,10},{10,1... | collective-permute-start | bytes 221192 | tf_op jit(solution)/shard_map/ppermute | solution.py:18
  28.6 24.9 %collective-permute-start.9 = (f32[9,1,2048]{2,0,1:T(8,128)S(1)}, f32[9,1,2048]{2,0,1:T(8,128)S(1)}, u32[]{:S(2)}, u32[]{:S(2)}) collective-permute-start(f32[9,1,2048]{2,0,1:T(8,128)S(1)} %copy.131), channel_id=1, source_target_pairs={{0,31},{1,0},{2,1},{3,2},{4,3},{5,4},{6,5},{7,6},{8,7},{9,8},{10,9... | collective-permute-start | bytes 221192 | tf_op jit(solution)/shard_map/ppermute | solution.py:18
  40.8 2.6 %collective-permute-start.4 = (f32[9,1,2048]{2,0,1:T(8,128)S(1)}, f32[9,1,2048]{2,0,1:T(8,128)S(1)}, u32[]{:S(2)}, u32[]{:S(2)}) collective-permute-start(f32[9,1,2048]{2,0,1:T(8,128)S(1)} %get-tuple-element.71), channel_id=1, source_target_pairs={{0,31},{1,0},{2,1},{3,2},{4,3},{5,4},{6,5},{7,6},{8,7},{9,8},{10,9... | collective-permute-start | bytes 221192 | tf_op jit(solution)/shard_map/ppermute | solution.py:18
  40.8 8.2 %collective-permute-start.5 = (f32[9,1,2048]{2,0,1:T(8,128)S(1)}, f32[9,1,2048]{2,0,1:T(8,128)S(1)}, u32[]{:S(2)}, u32[]{:S(2)}) collective-permute-start(f32[9,1,2048]{2,0,1:T(8,128)S(1)} %get-tuple-element.72), channel_id=1, source_target_pairs={{0,1},{1,2},{2,3},{3,4},{4,5},{5,6},{6,7},{7,8},{8,9},{9,10},{10,1... | collective-permute-start | bytes 221192 | tf_op jit(solution)/shard_map/ppermute | solution.py:18
  56.7 8.0 %collective-permute-start.10 = (f32[9,1,2048]{2,0,1:T(8,128)S(1)}, f32[9,1,2048]{2,0,1:T(8,128)S(1)}, u32[]{:S(2)}, u32[]{:S(2)}) collective-permute-start(f32[9,1,2048]{2,0,1:T(8,128)S(1)} %copy.141), channel_id=1, source_target_pairs={{0,1},{1,2},{2,3},{3,4},{4,5},{5,6},{6,7},{7,8},{8,9},{9,10},{10,1... | collective-permute-start | bytes 221192 | tf_op jit(solution)/shard_map/ppermute | solution.py:18
  56.8 7.9 %collective-permute-start.11 = (f32[9,1,2048]{2,0,1:T(8,128)S(1)}, f32[9,1,2048]{2,0,1:T(8,128)S(1)}, u32[]{:S(2)}, u32[]{:S(2)}) collective-permute-start(f32[9,1,2048]{2,0,1:T(8,128)S(1)} %copy.142), channel_id=1, source_target_pairs={{0,31},{1,0},{2,1},{3,2},{4,3},{5,4},{6,5},{7,6},{8,7},{9,8},{10,9... | collective-permute-start | bytes 221192 | tf_op jit(solution)/shard_map/ppermute | solution.py:18
  62.3 4.3 %collective-permute-start.6 = (f32[9,1,2048]{2,0,1:T(8,128)S(1)}, f32[9,1,2048]{2,0,1:T(8,128)S(1)}, u32[]{:S(2)}, u32[]{:S(2)}) collective-permute-start(f32[9,1,2048]{2,0,1:T(8,128)S(1)} %get-tuple-element.68), channel_id=1, source_target_pairs={{0,31},{1,0},{2,1},{3,2},{4,3},{5,4},{6,5},{7,6},{8,7},{9,8},{10,9... | collective-permute-start | bytes 221192 | tf_op jit(solution)/shard_map/ppermute | solution.py:18
  62.3 8.0 %collective-permute-start.7 = (f32[9,1,2048]{2,0,1:T(8,128)S(1)}, f32[9,1,2048]{2,0,1:T(8,128)S(1)}, u32[]{:S(2)}, u32[]{:S(2)}) collective-permute-start(f32[9,1,2048]{2,0,1:T(8,128)S(1)} %get-tuple-element.69), channel_id=1, source_target_pairs={{0,1},{1,2},{2,3},{3,4},{4,5},{5,6},{6,7},{7,8},{8,9},{9,10},{10,1... | collective-permute-start | bytes 221192 | tf_op jit(solution)/shard_map/ppermute | solution.py:18
  71.7 8.0 %collective-permute-start.12 = (f32[9,1,2048]{2,0,1:T(8,128)S(1)}, f32[9,1,2048]{2,0,1:T(8,128)S(1)}, u32[]{:S(2)}, u32[]{:S(2)}) collective-permute-start(f32[9,1,2048]{2,0,1:T(8,128)S(1)} %copy.152), channel_id=1, source_target_pairs={{0,1},{1,2},{2,3},{3,4},{4,5},{5,6},{6,7},{7,8},{8,9},{9,10},{10,1... | collective-permute-start | bytes 221192 | tf_op jit(solution)/shard_map/ppermute | solution.py:18
  71.8 7.9 %collective-permute-start.13 = (f32[9,1,2048]{2,0,1:T(8,128)S(1)}, f32[9,1,2048]{2,0,1:T(8,128)S(1)}, u32[]{:S(2)}, u32[]{:S(2)}) collective-permute-start(f32[9,1,2048]{2,0,1:T(8,128)S(1)} %copy.153), channel_id=1, source_target_pairs={{0,31},{1,0},{2,1},{3,2},{4,3},{5,4},{6,5},{7,6},{8,7},{9,8},{10,9... | collective-permute-start | bytes 221192 | tf_op jit(solution)/shard_map/ppermute | solution.py:18
  82.7 8.1 %collective-permute-start.14 = (f32[9,1,2048]{2,0,1:T(8,128)S(1)}, f32[9,1,2048]{2,0,1:T(8,128)S(1)}, u32[]{:S(2)}, u32[]{:S(2)}) collective-permute-start(f32[9,1,2048]{2,0,1:T(8,128)S(1)} %copy.163), channel_id=1, source_target_pairs={{0,1},{1,2},{2,3},{3,4},{4,5},{5,6},{6,7},{7,8},{8,9},{9,10},{10,1... | collective-permute-start | bytes 221192 | tf_op jit(solution)/shard_map/ppermute | solution.py:18
  82.8 8.0 %collective-permute-start.15 = (f32[9,1,2048]{2,0,1:T(8,128)S(1)}, f32[9,1,2048]{2,0,1:T(8,128)S(1)}, u32[]{:S(2)}, u32[]{:S(2)}) collective-permute-start(f32[9,1,2048]{2,0,1:T(8,128)S(1)} %copy.164), channel_id=1, source_target_pairs={{0,31},{1,0},{2,1},{3,2},{4,3},{5,4},{6,5},{7,6},{8,7},{9,8},{10,9... | collective-permute-start | bytes 221192 | tf_op jit(solution)/shard_map/ppermute | solution.py:18
where the time goes:
time: 94.5 us; the launch traced here: 94.1 us
  starting transfers between devices  30 us (32%)
  waiting for transfers between devices  25.1 us (27%)
  other arithmetic  15.9 us (17%)
  local copies, waits for them, and re-layouts  13.3 us (14%)
  matrix products  7.25 us (8%)
  between operations  2.71 us (3%)
    ppermute x16, starting transfers between devices, passed_along(): lax.ppermute(x, axis, [(i, (i + by) % devices) for i in range(devices)])  30 us
    ppermute x16, waiting for transfers between devices, passed_along(): lax.ppermute(x, axis, [(i, (i + by) % devices) for i in range(devices)])  25.1 us
    unnamed x52, local copies, waits for them, and re-layouts  6.99 us
    dot_general x8, matrix products, collide(): jnp.einsum('iq,qxs->ixs', velocity, bulk_velocity, precision=lax.Precisio...  3.86 us
    rev x8, local copies, waits for them, and re-layouts, collide(): return jnp.where(solid[None] == 1, populations[::-1], relaxed)  3.59 us
    reduce_sum x12, other arithmetic, collide(): excess = jnp.sum(blended * logged, axis=0) - entropy  3.59 us
    dot_general x8, matrix products, collide(): jnp.einsum('iq,ixs->qxs', velocity, populations, precision=lax.Precision....  3.39 us
    unnamed x56, other arithmetic  3.31 us
  transfers between devices with their start and end apart: 16, of which 9 were waited for; matrix products, arithmetic and copies ran while one was open for 15% of the time, Pallas kernels for 0%

commit v1 on v0

v1 whole, which is shorter than its diff:
```python
import functools

import jax
import jax.numpy as jnp
from jax import lax
from jax.experimental import pallas as pl
from jax.experimental.pallas import tpu as pltpu
from jax.sharding import PartitionSpec as P

NZ = 128
NEWTON = 3
BETA = 0.85
AXIS = "gx"

OUT, MID, IN = 0, 1, 2
SCALE = 1.0 / 216.0
LEVELS = (216.0 * 8.0 / 27.0, 216.0 * 2.0 / 27.0, 216.0 / 54.0, 1.0)


def level(a, b, c):
    return abs(a - 1) + abs(b - 1) + abs(c - 1)


CLASSES = [[(a, b, c) for a in range(3) for b in range(3) for c in range(3) if level(a, b, c) == n] for n in range(4)]
EVERY = [d for group in CLASSES for d in group]


def slot(d):
    return d[0] * 9 + d[1] * 3 + d[2]


def opposite(d):
    return (2 - d[0], 2 - d[1], 2 - d[2])


def moved(x, b, c, sign):
    shift_y, shift_z = (sign * (b - 1)) % x.shape[0], (sign * (c - 1)) % x.shape[1]
    if shift_y:
        x = pltpu.roll(x, shift_y, 0)
    if shift_z:
        x = pltpu.roll(x, shift_z, 1)
    return x


def odd_device():
    return lax.rem(lax.axis_index(AXIS), 2)


def facing(odd):
    return 1.0 - 2.0 * odd.astype(jnp.float32)


def block_of(a, odd):
    return (a + odd * (2 - 2 * a)) * 9


def moments(get, second):
    along = []
    for a in range(3):
        rows = []
        for b in range(3):
            low, zero, high = get((a, b, 0)), get((a, b, 1)), get((a, b, 2))
            both = low + high
            rows.append((4.0 * zero + both, high - low, both))
        (l0, l1, l2), (z0, z1, z2), (h0, h1, h2) = rows
        edge = l0 + h0
        parts = [4.0 * z0 + edge, h0 - l0, 4.0 * z1 + (l1 + h1)]
        if second:
            parts += [edge, h1 - l1, 4.0 * z2 + (l2 + h2)]
        along.append(parts)
    low, zero, high = along

    def even(n):
        return 4.0 * zero[n] + (low[n] + high[n])

    result = [even(0), high[0] - low[0], even(1), even(2)]
    if second:
        result += [low[0] + high[0], even(3), even(5), high[1] - low[1], high[2] - low[2], even(4)]
    return result


def weighted(term):
    totals = None
    for group, weight in zip(CLASSES, LEVELS):
        sums = None
        for d in group:
            values = term(d)
            sums = list(values) if sums is None else [s + v for s, v in zip(sums, values)]
        sums = [weight * s for s in sums]
        totals = sums if totals is None else [t + s for t, s in zip(totals, sums)]
    return totals


def collide(get, force, solid, newton, offset, emit):
    mass, mx, my, mz = moments(get, False)
    density = SCALE * mass
    ux = (SCALE * mx + force[0]) / density
    uy = (SCALE * my + force[1]) / density
    uz = (SCALE * mz + force[2]) / density
    base = density * (1.0 - 1.5 * (ux * ux + uy * uy + uz * uz))
    linear, square = 3.0 * density, 4.5 * density
    projected = {}
    for d in EVERY:
        if d == (1, 1, 1) or opposite(d) in projected:
            continue
        total = None
        for speed, u in zip(d, (ux, uy, uz)):
            if speed == 1:
                continue
            if total is None:
                total, flip = u, speed
            else:
                total = total + u if speed == flip else total - u
        projected[d] = None
        even = base + square * total * total
        tilt = linear * total
        up, down = (d, opposite(d)) if flip == 2 else (opposite(d), d)
        offset[slot(up)] = (even + tilt) - get(up)
        offset[slot(down)] = (even - tilt) - get(down)
    offset[slot((1, 1, 1))] = base - get((1, 1, 1))

    reach = None

    def first(d):
        nonlocal reach
        value, step = get(d), offset[slot(d)]
        limit = jnp.where(step < 0.0, value / jnp.maximum(-step, 0.001), 1000000000.0)
        reach = limit if reach is None else jnp.minimum(reach, limit)
        return value * jnp.log(value), step

    entropy, drift = weighted(first)
    cap = jnp.clip(0.9 * reach, 1.0, 2.0)
    factor = cap
    for k in range(NEWTON):

        def term(d, factor=factor):
            step = offset[slot(d)]
            mixed = get(d) + factor * step
            logged = jnp.log(mixed)
            return mixed * logged, step * logged, step * step / mixed

        mixing, slope, bend = weighted(term)
        update = factor - (mixing - entropy) / jnp.maximum(slope + drift, 0.5 * bend)
        factor = jnp.where(newton > k, jnp.clip(update, 1.0, cap), factor)
    rate = BETA * factor
    for d in EVERY:
        emit(d, lambda d=d: jnp.where(solid == 1, get(opposite(d)), get(d) + rate * offset[slot(d)]))
    return ux, uy, uz, jnp.where(solid == 1, 0.0, rate)


def pull_back(get, saved, solid, emit):
    ux, uy, uz, rate = saved
    total, vx, vy, vz, txx, tyy, tzz, txy, txz, tyz = [SCALE * m for m in moments(get, True)]
    sx = txx * ux + txy * uy + txz * uz
    sy = txy * ux + tyy * uy + tyz * uz
    sz = txz * ux + tyz * uy + tzz * uz
    hx = 3.0 * vx + 9.0 * sx - 3.0 * ux * total
    hy = 3.0 * vy + 9.0 * sy - 3.0 * uy * total
    hz = 3.0 * vz + 9.0 * sz - 3.0 * uz * total
    grown = (
        total * (1.0 - 1.5 * (ux * ux + uy * uy + uz * uz))
        + 3.0 * (vx * ux + vy * uy + vz * uz)
        + 4.5 * (sx * ux + sy * uy + sz * uz)
    )
    px, py, pz = rate * hx, rate * hy, rate * hz
    kept = rate * (grown - (hx * ux + hy * uy + hz * uz))
    stay = 1.0 - rate
    for a in range(3):
        at_a = kept + (a - 1) * px if a != 1 else kept
        for b in range(3):
            at_b = at_a + (b - 1) * py if b != 1 else at_a
            for c in range(3):
                d = (a, b, c)
                shared = at_b + (c - 1) * pz if c != 1 else at_b
                emit(d, lambda d=d, shared=shared: jnp.where(solid == 1, get(opposite(d)), stay * get(d) + shared))
    return px, py, pz


def reader(*blocks):
    def get(d):
        ref, start = blocks[d[0]]
        return ref[start + d[1] * 3 + d[2]]

    return get


def writer(sign, **targets):
    table = {OUT: targets.get("out"), MID: targets.get("mid"), IN: targets.get("into")}

    def emit(d, value):
        if table[d[0]] is None:
            return
        ref, start = table[d[0]]
        ref[start + d[1] * 3 + d[2]] = moved(value(), d[1], d[2], sign)

    return emit


def keep(ref, values):
    for n, value in enumerate(values):
        ref[n] = value


def saved_of(ref):
    return tuple(ref[n] for n in range(4))


def framed(force, at=0):
    return facing(odd_device()) * force[at], force[at + 1], force[at + 2]


def first_kernel(start, force, solid, newton, inward, outward, saved, scaled, offset):
    odd = odd_device()
    for d in EVERY:
        scaled[slot(d)] = (216.0 / LEVELS[level(*d)]) * start[block_of(d[0], odd) + d[1] * 3 + d[2]]
    get = reader((scaled, 0), (scaled, 9), (scaled, 18))
    keep(saved, collide(get, framed(force), solid[...], newton[...], offset, writer(1, into=(inward, 0), out=(outward, 0), mid=(outward, 9))))
    for n in range(3):
        outward[18 + n] = force[n]
    outward[21] = solid[...].astype(jnp.float32)
    outward[22] = newton[...].astype(jnp.float32)


def own_kernel(at, f_in, f_mid, f_out, force, solid, newton, inward, local, saved, offset):
    get = reader((f_out, at[OUT]), (f_mid, at[MID]), (f_in, at[IN]))
    keep(saved, collide(get, framed(force), solid[...], newton[...], offset, writer(1, into=(inward, 0), mid=(local, 0), out=(local, 9))))


def ghost_kernel(at, f_in, f_mid, f_out, cells, local, saved, offset):
    get = reader((f_out, at[OUT]), (f_mid, at[MID]), (f_in, at[IN]))
    keep(saved, collide(get, framed(cells, 18), cells[21], cells[22], offset, writer(1, into=(local, 0), mid=(local, 9))))


def cotangent_kernel(cotangent, after, outward, inward):
    odd = odd_device()
    for d in EVERY:
        value = cotangent[block_of(d[0], odd) + d[1] * 3 + d[2]]
        ref, start = ((outward, 0), (inward, 9), (inward, 0))[d[0]]
        ref[start + d[1] * 3 + d[2]] = moved(value, d[1], d[2], -1)


def turn_own_kernel(f_in, f_mid, f_out, force, solid, newton, m_in, m_mid, m_out, inward, final_mid, outward, local, push, offset):
    get = reader((f_out, 0), (f_mid, 0), (f_in, 0))
    saved = collide(get, framed(force), solid[...], newton[...], offset, writer(1, into=(inward, 0), mid=(final_mid, 0)))
    from_above = reader((m_out, 0), (m_mid, 9), (m_in, 0))
    keep(push, pull_back(from_above, saved, solid[...], writer(-1, out=(outward, 0), into=(local, 0), mid=(local, 9))))


def turn_ghost_kernel(f_in, f_mid, f_out, cells, m_in, m_mid, m_out, final_in, local, offset):
    get = reader((f_out, 9), (f_mid, 9), (f_in, 0))
    saved = collide(get, framed(cells, 18), cells[21], cells[22], offset, writer(1, into=(final_in, 0)))
    from_above = reader((m_out, 0), (m_mid, 9), (m_in, 0))
    pull_back(from_above, saved, cells[21], writer(-1, out=(local, 0), mid=(local, 9)))


def back_own_kernel(m_in, m_mid, m_out, saved, solid, push, outward, local, push_out):
    get = reader((m_out, 0), (m_mid, 9), (m_in, 0))
    terms = pull_back(get, saved_of(saved), solid[...], writer(-1, out=(outward, 0), into=(local, 0), mid=(local, 9)))
    for n in range(3):
        push_out[n] = push[n] + terms[n]


def back_ghost_kernel(m_in, m_mid, m_out, saved, cells, local):
    get = reader((m_out, 0), (m_mid, 9), (m_in, 0))
    pull_back(get, saved_of(saved), cells[21], writer(-1, out=(local, 0), mid=(local, 9)))


def last_kernel(m_in, m_mid, m_out, saved, solid, push, grad, grad_push):
    odd = odd_device()

    def emit(d, value):
        grad[block_of(d[0], odd) + d[1] * 3 + d[2]] = value()

    get = reader((m_out, 0), (m_mid, 9), (m_in, 0))
    terms = pull_back(get, saved_of(saved), solid[...], emit)
    grad_push[0] = facing(odd) * (push[0] + terms[0])
    grad_push[1] = push[1] + terms[1]
    grad_push[2] = push[2] + terms[2]


def final_kernel(f_in, f_mid, f_out, ratio):
    odd = odd_device()
    for a, ref in ((OUT, f_out), (MID, f_mid), (IN, f_in)):
        start = block_of(a, odd)
        for n in range(9):
            ratio[start + n] = ref[n]


def call(kernel, outs, *args, scratch=(27,), flops=4000000):
    plane = args[0].shape[1:]
    return pl.pallas_call(
        kernel,
        out_shape=[jax.ShapeDtypeStruct((n,) + plane, jnp.float32) for n in outs],
        scratch_shapes=[pltpu.VMEM((n,) + plane, jnp.float32) for n in scratch],
        compiler_params=pltpu.CompilerParams(vmem_limit_bytes=8 * 1024 * 1024),
        cost_estimate=pl.CostEstimate(flops=flops, bytes_accessed=1000000, transcendentals=0),
    )(*args)


def on_device(populations0, force, solid, newton, cotangent):
    devices = lax.axis_size(AXIS)
    rows = populations0.shape[2] // NZ

    def planes(x):
        return x.reshape(x.shape[:-2] + (rows, NZ))

    def partner(x):
        return lax.ppermute(x, AXIS, [(i, i ^ 1) for i in range(devices)])

    def inward_two(x):
        return lax.ppermute(x, AXIS, [(i, (i + 2 - 4 * (i % 2)) % devices) for i in range(devices)])

    def outward_one(x):
        return lax.ppermute(x, AXIS, [(i, (i - 1 + 2 * (i % 2)) % devices) for i in range(devices)])

    def outward_two(x):
        return inward_two(x)

    start, force, cotangent = planes(populations0), planes(force), planes(cotangent)
    solid, newton = solid.reshape(rows, NZ), newton.reshape(rows, NZ)
    cells = (force, solid, newton)

    inward, beside, saved0 = call(first_kernel, (9, 23, 4), start, *cells, scratch=(27, 27))
    far, near, ghost = inward_two(inward), partner(inward), outward_one(beside)
    inward, own1, saved1 = call(
        functools.partial(own_kernel, (0, 9, 0)), (9, 18, 4), ghost, beside, near, *cells
    )
    near1, far1 = partner(inward), inward_two(inward)
    ghost1, saved_ghost1 = call(functools.partial(ghost_kernel, (0, 9, 0)), (18, 4), far, ghost, beside, ghost)
    cot_out, cot_in = call(cotangent_kernel, (9, 18), cotangent, ghost1, scratch=(), flops=200000)
    inward, own2, saved2 = call(functools.partial(own_kernel, (0, 0, 0)), (9, 18, 4), ghost1, own1, near1, *cells)
    near2, far2 = partner(inward), inward_two(inward)
    cot_near, cot_far, cot_ghost = partner(cot_out), outward_two(cot_out), outward_one(cot_in)
    ghost2, saved_ghost2 = call(functools.partial(ghost_kernel, (9, 9, 0)), (18, 4), far1, ghost1, own1, ghost)
    last_in, last_mid, out3, own3, push = call(
        turn_own_kernel, (9, 9, 9, 18, 3), ghost2, own2, near2, *cells, cot_near, cot_in, cot_ghost
    )
    near3, far3 = partner(out3), outward_two(out3)
    last_ghost, ghost3 = call(
        turn_ghost_kernel, (9, 18), far2, ghost2, own2, ghost, cot_in, cot_ghost, cot_far
    )
    out2, own_b2, push = call(back_own_kernel, (9, 18, 3), near3, own3, ghost3, saved2, solid, push, scratch=(), flops=800000)
    near_b2, far_b2 = partner(out2), outward_two(out2)
    (ghost_b2,) = call(back_ghost_kernel, (18,), own3, ghost3, far3, saved_ghost2, ghost, scratch=(), flops=800000)
    out1, own_b1, push = call(back_own_kernel, (9, 18, 3), near_b2, own_b2, ghost_b2, saved1, solid, push, scratch=(), flops=800000)
    near_b1 = partner(out1)
    (ghost_b1,) = call(back_ghost_kernel, (18,), own_b2, ghost_b2, far_b2, saved_ghost1, ghost, scratch=(), flops=800000)
    grad, grad_push = call(last_kernel, (27, 3), near_b1, own_b1, ghost_b1, saved0, solid, push, scratch=(), flops=800000)
    last_near = partner(last_in)
    (ratio,) = call(final_kernel, (27,), last_ghost, last_mid, last_near, scratch=(), flops=200000)
    return (ratio.reshape(populations0.shape), grad.reshape(populations0.shape), grad_push.reshape(3, 1, rows * NZ))


def solution(mesh):
    return jax.shard_map(
        on_device,
        mesh=mesh,
        in_specs=(P(None, AXIS, None), P(None, AXIS, None), P(AXIS, None), P(AXIS, None), P(None, AXIS, None)),
        out_specs=(P(None, AXIS, None), P(None, AXIS, None), P(None, AXIS, None)),
        check_vma=False,
    )
```

time: 94.5 us -> 48.3 us (0.51)
  other arithmetic: 15.9 us -> 0 us
  starting transfers between devices: 30 us -> 15 us
  local copies, waits for them, and re-layouts: 13.3 us -> 3.09 us
  matrix products: 7.25 us -> 0 us
  Pallas kernels: 0 us -> 6.26 us
  waiting for transfers between devices: 25.1 us -> 22.9 us
  between operations: 2.71 us -> 0.84 us
    ppermute x16, starting transfers between devices: 30 us -> 15 us  [the longest x2 8.89 us: outward_one(): lax.ppermute(x, AXIS, [(i, (i - 1 + 2 * (i % 2)) % devices) for i in rang...]
    dot_general x16 -> x0, matrix products: 7.25 us -> none  [the longest x8 3.86 us: collide(): jnp.einsum('iq,qxs->ixs', velocity, bulk_velocity, precision=lax.Precisio...]
    reduce_sum x44 -> x0, other arithmetic: 7.13 us -> none  [the longest x12 3.59 us: collide(): excess = jnp.sum(blended * logged, axis=0) - entropy]
    pallas_call x0 -> x14, Pallas kernels: none -> 6.26 us  [call(): pl.pallas_call(kernel, out_shape=[jax.ShapeDtypeStruct((n,) + plane, jnp....]
    unnamed x52 -> x16, local copies, waits for them, and re-layouts: 6.99 us -> 3.09 us
    rev x8 -> x0, local copies, waits for them, and re-layouts: 3.59 us -> none  [collide(): return jnp.where(solid[None] == 1, populations[::-1], relaxed)]
    unnamed x56 -> x0, other arithmetic: 3.31 us -> none
    concatenate x36 -> x0, other arithmetic: 2.67 us -> none  [the longest x32 2.51 us: plane_rolls(): jnp.roll(member, (sign * along_y, sign * along_z), axis=(2, 3))]
  transfers between devices with their start and end apart: 16 -> 16, of which waited for: 9 -> 8; matrix products, arithmetic and copies ran while one was open for 15% -> 0% of each run, Pallas kernels for 0% -> 10%
where the time goes in v1:
time: 48.3 us; the launch traced here: 48 us
  waiting for transfers between devices  22.9 us (47%)
  starting transfers between devices  15 us (31%)
  Pallas kernels  6.26 us (13%)
  local copies, waits for them, and re-layouts  3.09 us (6%)
  between operations  0.84 us (2%)
    ppermute x6, waiting for transfers between devices, inward_two(): lax.ppermute(x, AXIS, [(i, (i + 2 - 4 * (i % 2)) % devices) for i in rang...  19 us
    ppermute x2, starting transfers between devices, outward_one(): lax.ppermute(x, AXIS, [(i, (i - 1 + 2 * (i % 2)) % devices) for i in rang...  8.89 us
    pallas_call x14, Pallas kernels, call(): pl.pallas_call(kernel, out_shape=[jax.ShapeDtypeStruct((n,) + plane, jnp....  6.26 us
    ppermute x8, starting transfers between devices, partner(): return lax.ppermute(x, AXIS, [(i, i ^ 1) for i in range(devices)])  6 us
    unnamed x16, local copies, waits for them, and re-layouts  3.09 us
    ppermute x2, waiting for transfers between devices, outward_one(): lax.ppermute(x, AXIS, [(i, (i - 1 + 2 * (i % 2)) % devices) for i in rang...  2.63 us
    ppermute x8, waiting for transfers between devices, partner(): return lax.ppermute(x, AXIS, [(i, i ^ 1) for i in range(devices)])  1.28 us
  transfers between devices with their start and end apart: 16, of which 8 were waited for; matrix products, arithmetic and copies ran while one was open for 0% of the time, Pallas kernels for 10%

profile of v1, /device:TPU:0, one launch (start us, length us, event | category | flops | bytes accessed | tf_op | source)
XLA Modules:
  0.0 48.0 jit_solution(15878973924492755534)
XLA Ops:
  0.6 0.0 copy-start
  0.6 0.7 %copy-done = s32[1,2048]{1,0:T(1,128)S(1)} copy-done((s32[1,2048]{1,0:T(1,128)S(1)}, s32[1,2048]{1,0:T(1,128)}, u32[]{:S(2)}) %copy-start) | copy-done | bytes 8216
  1.3 0.0 copy-start.2
  1.3 0.7 %copy-done.2 = f32[3,1,2048]{2,1,0:T(1,128)S(1)} copy-done((f32[3,1,2048]{2,1,0:T(1,128)S(1)}, f32[3,1,2048]{2,1,0:T(1,128)}, u32[]{:S(2)}) %copy-start.2) | copy-done | bytes 24600
  2.1 0.0 copy-start.4
  2.1 0.9 %copy-done.4 = f32[27,1,2048]{2,1,0:T(1,128)S(1)} copy-done((f32[27,1,2048]{2,1,0:T(1,128)S(1)}, f32[27,1,2048]{2,1,0:T(1,128)}, u32[]{:S(2)}) %copy-start.4) | copy-done | bytes 221208
  3.0 0.0 copy-start.6
  3.0 0.7 %copy-done.6 = s32[1,2048]{1,0:T(1,128)S(1)} copy-done((s32[1,2048]{1,0:T(1,128)S(1)}, s32[1,2048]{1,0:T(1,128)}, u32[]{:S(2)}) %copy-start.6) | copy-done | bytes 8216
  3.7 0.6 %shard_map.76 = (f32[9,16,128]{2,1,0:T(8,128)S(1)}, f32[23,16,128]{2,1,0:T(8,128)S(1)}, f32[4,16,128]{2,1,0:T(8,128)S(1)}) custom-call(f32[27,16,128]{2,1,0:T(8,128)S(1)} %bitcast.19, f32[3,16,128]{2,1,0:T(8,128)S(1)} %bitcast.15, s32[16,128]{1,0:T(8,128)S(1)} %bitcast.8, s32[16,128]{1,0:T(8,128)S(1)} %bitcast.21), custom_call_target="tpu_custom_call" | custom-call | flops 4000000 | bytes 1000000 | tf_op jit(solution)/shard_map/pallas_call | solution.py:291
  4.3 6.5 %collective-permute-start.1 = (f32[23,16,128]{2,1,0:T(8,128)S(1)}, f32[23,16,128]{2,1,0:T(8,128)S(1)}, u32[]{:S(2)}, u32[]{:S(2)}) collective-permute-start(f32[23,16,128]{2,1,0:T(8,128)S(1)} %get-tuple-element.34.f_out.f_mid), channel_id=1, source_target_pairs={{0,31},{1,2},{2,1},{3,4},{4,3},{5,6},{6,5},{7,8},{8,7},{9,10},{10,... | collective-permute-start | bytes 565256 | tf_op jit(solution)/shard_map/ppermute | solution.py:314
  10.8 0.0 collective-permute-start.2
  10.8 0.0 collective-permute-start
  10.8 1.3 %collective-permute-done.2.f_out = f32[9,16,128]{2,1,0:T(8,128)S(1)} collective-permute-done((f32[9,16,128]{2,1,0:T(8,128)S(1)}, f32[9,16,128]{2,1,0:T(8,128)S(1)}, u32[]{:S(2)}, u32[]{:S(2)}) %collective-permute-start.2) | collective-permute-done | bytes 73760 | tf_op jit(solution)/shard_map/ppermute | solution.py:308
  12.1 2.6 %collective-permute-done.1.f_mid.cells.f_in = f32[23,16,128]{2,1,0:T(8,128)S(1)} collective-permute-done((f32[23,16,128]{2,1,0:T(8,128)S(1)}, f32[23,16,128]{2,1,0:T(8,128)S(1)}, u32[]{:S(2)}, u32[]{:S(2)}) %collective-permute-start.1) | collective-permute-done | bytes 188448 | tf_op jit(solution)/shard_map/ppermute | solution.py:314
  14.7 0.6 %shard_map.78 = (f32[9,16,128]{2,1,0:T(8,128)S(1)}, f32[18,16,128]{2,1,0:T(8,128)S(1)}, f32[4,16,128]{2,1,0:T(8,128)S(1)}) custom-call(f32[23,16,128]{2,1,0:T(8,128)S(1)} %collective-permute-done.1.f_mid.cells.f_in, f32[23,16,128]{2,1,0:T(8,128)S(1)} %get-tuple-element.34.f_out.f_mid, f32[9,16,128]{2,1,0:T(8,128)S(1)} %collective-permute-done.2.f_out, ...), custom_call_target="tpu_custom_call" | custom-call | flops 4000000 | bytes 1000000 | tf_op jit(solution)/shard_map/pallas_call | solution.py:291
  15.3 0.0 copy-start.5
  15.3 0.1 collective-permute-start.3
  15.4 3.4 %collective-permute-done.f_in = f32[9,16,128]{2,1,0:T(8,128)S(1)} collective-permute-done((f32[9,16,128]{2,1,0:T(8,128)S(1)}, f32[9,16,128]{2,1,0:T(8,128)S(1)}, u32[]{:S(2)}, u32[]{:S(2)}) %collective-permute-start) | collective-permute-done | bytes 73760 | tf_op jit(solution)/shard_map/ppermute | solution.py:311
  18.8 0.6 %shard_map.77 = (f32[18,16,128]{2,1,0:T(8,128)S(1)}, f32[4,16,128]{2,1,0:T(8,128)S(1)}) custom-call(f32[9,16,128]{2,1,0:T(8,128)S(1)} %collective-permute-done.f_in, f32[23,16,128]{2,1,0:T(8,128)S(1)} %collective-permute-done.1.f_mid.cells.f_in, f32[23,16,128]{2,1,0:T(8,128)S(1)} %get-tuple-element.34.f_out.f_mid, ...), custom_call_target="tpu_custom_call" | custom-call | flops 4000000 | bytes 1000000 | tf_op jit(solution)/shard_map/pallas_call | solution.py:291
  19.3 0.0 copy-done.5
  19.3 0.0 copy-start.1
  19.3 0.0 copy-start.3
  19.3 0.0 copy-start.7
  19.4 0.1 shard_map.81
  19.5 2.4 %collective-permute-start.6 = (f32[18,16,128]{2,1,0:T(8,128)S(1)}, f32[18,16,128]{2,1,0:T(8,128)S(1)}, u32[]{:S(2)}, u32[]{:S(2)}) collective-permute-start(f32[18,16,128]{2,1,0:T(8,128)S(1)} %get-tuple-element.41.m_in.m_mid), channel_id=1, source_target_pairs={{0,31},{1,2},{2,1},{3,4},{4,3},{5,6},{6,5},{7,8},{8,7},{9,10},{10,... | collective-permute-start | bytes 442376 | tf_op jit(solution)/shard_map/ppermute | solution.py:314
  21.9 0.0 collective-permute-start.5
  21.9 3.1 %collective-permute-start.9 = (f32[9,16,128]{2,1,0:T(8,128)S(1)}, f32[9,16,128]{2,1,0:T(8,128)S(1)}, u32[]{:S(2)}, u32[]{:S(2)}) collective-permute-start(f32[9,16,128]{2,1,0:T(8,128)S(1)} %get-tuple-element.42), channel_id=1, source_target_pairs={{0,1},{1,0},{2,3},{3,2},{4,5},{5,4},{6,7},{7,6},{8,9},{9,8},{10,11... | collective-permute-start | bytes 221192 | tf_op jit(solution)/shard_map/ppermute | solution.py:308
  25.0 0.0 collective-permute-done.3.f_out
  25.0 0.0 copy-done.1
  25.0 0.0 copy-done.3
  25.0 0.0 copy-done.7
  25.0 0.6 %shard_map.79 = (f32[9,16,128]{2,1,0:T(8,128)S(1)}, f32[18,16,128]{2,1,0:T(8,128)S(1)}, f32[4,16,128]{2,1,0:T(8,128)S(1)}) custom-call(f32[18,16,128]{2,1,0:T(8,128)S(1)} %get-tuple-element.35.f_in.f_mid.after, f32[18,16,128]{2,1,0:T(8,128)S(1)} %get-tuple-element.36.f_mid.f_out, f32[9,16,128]{2,1,0:T(8,128)S(1)} %collective-permute-done.3.f_out, ...), custom_call_target="tpu_custom_call" | custom-call | flops 4000000 | bytes 1000000 | tf_op jit(solution)/shard_map/pallas_call | solution.py:291
  25.6 0.1 collective-permute-start.8
  25.7 0.1 collective-permute-start.7
  25.7 4.1 %collective-permute-done.5.f_in = f32[9,16,128]{2,1,0:T(8,128)S(1)} collective-permute-done((f32[9,16,128]{2,1,0:T(8,128)S(1)}, f32[9,16,128]{2,1,0:T(8,128)S(1)}, u32[]{:S(2)}, u32[]{:S(2)}) %collective-permute-start.5) | collective-permute-done | bytes 73760 | tf_op jit(solution)/shard_map/ppermute | solution.py:311
  29.8 0.0 collective-permute-start.4
  29.8 0.5 %shard_map.80 = (f32[18,16,128]{2,1,0:T(8,128)S(1)}, f32[4,16,128]{2,1,0:T(8,128)S(1)}) custom-call(f32[9,16,128]{2,1,0:T(8,128)S(1)} %collective-permute-done.5.f_in, f32[18,16,128]{2,1,0:T(8,128)S(1)} %get-tuple-element.35.f_in.f_mid.after, f32[18,16,128]{2,1,0:T(8,128)S(1)} %get-tuple-element.36.f_mid.f_out, ...), custom_call_target="tpu_custom_call" | custom-call | flops 4000000 | bytes 1000000 | tf_op jit(solution)/shard_map/pallas_call | solution.py:291
  30.4 0.0 collective-permute-done.9.m_in
  30.4 0.0 collective-permute-done.8.f_out
  30.4 0.0 collective-permute-done.6.m_mid.m_out
  30.4 0.6 %shard_map.83 = (f32[9,16,128]{2,1,0:T(8,128)S(1)}, f32[9,16,128]{2,1,0:T(8,128)S(1)}, f32[9,16,128]{2,1,0:T(8,128)S(1)}, f32[18,16,128]{2,1,0:T(8,128)S(1)}, f32[3,16,128]{2,1,0:T(8,128)S(1)}) custom-call(f32[18,16,128]{2,1,0:T(8,128)S(1)} %get-tuple-element.39.f_mid.f_in, f32[18,16,128]{2,1,0:T(8,128)S(1)} %get-tuple-element.40.f_out.f_mid, ...), custom_call_target="tpu_custom_call" | custom-call | flops 4000000 | bytes 1000000 | tf_op jit(solution)/shard_map/pallas_call | solution.py:291
  31.0 2.1 %collective-permute-start.11 = (f32[9,16,128]{2,1,0:T(8,128)S(1)}, f32[9,16,128]{2,1,0:T(8,128)S(1)}, u32[]{:S(2)}, u32[]{:S(2)}) collective-permute-start(f32[9,16,128]{2,1,0:T(8,128)S(1)} %get-tuple-element.46), channel_id=1, source_target_pairs={{0,1},{1,0},{2,3},{3,2},{4,5},{5,4},{6,7},{7,6},{8,9},{9,8},{10,11... | collective-permute-start | bytes 221192 | tf_op jit(solution)/shard_map/ppermute | solution.py:308
  33.2 0.0 collective-permute-start.13
  33.2 0.6 %collective-permute-done.7.m_out = f32[9,16,128]{2,1,0:T(8,128)S(1)} collective-permute-done((f32[9,16,128]{2,1,0:T(8,128)S(1)}, f32[9,16,128]{2,1,0:T(8,128)S(1)}, u32[]{:S(2)}, u32[]{:S(2)}) %collective-permute-start.7) | collective-permute-done | bytes 73760 | tf_op jit(solution)/shard_map/ppermute | solution.py:311
  33.8 4.0 %collective-permute-done.4.f_in = f32[9,16,128]{2,1,0:T(8,128)S(1)} collective-permute-done((f32[9,16,128]{2,1,0:T(8,128)S(1)}, f32[9,16,128]{2,1,0:T(8,128)S(1)}, u32[]{:S(2)}, u32[]{:S(2)}) %collective-permute-start.4) | collective-permute-done | bytes 73760 | tf_op jit(solution)/shard_map/ppermute | solution.py:311
  37.8 0.6 %shard_map.82 = (f32[9,16,128]{2,1,0:T(8,128)S(1)}, f32[18,16,128]{2,1,0:T(8,128)S(1)}) custom-call(f32[9,16,128]{2,1,0:T(8,128)S(1)} %collective-permute-done.4.f_in, f32[18,16,128]{2,1,0:T(8,128)S(1)} %get-tuple-element.39.f_mid.f_in, f32[18,16,128]{2,1,0:T(8,128)S(1)} %get-tuple-element.40.f_out.f_mid, ...), custom_call_target="tpu_custom_call" | custom-call | flops 4000000 | bytes 1000000 | tf_op jit(solution)/shard_map/pallas_call | solution.py:291
  38.4 0.0 collective-permute-done.11.m_in
  38.4 0.2 shard_map.85
  38.5 0.1 collective-permute-start.12
  38.6 0.5 %collective-permute-start.10 = (f32[9,16,128]{2,1,0:T(8,128)S(1)}, f32[9,16,128]{2,1,0:T(8,128)S(1)}, u32[]{:S(2)}, u32[]{:S(2)}) collective-permute-start(f32[9,16,128]{2,1,0:T(8,128)S(1)} %get-tuple-element.45), channel_id=1, source_target_pairs={{0,1},{1,0},{2,3},{3,2},{4,5},{5,4},{6,7},{7,6},{8,9},{9,8},{10,11... | collective-permute-start | bytes 221192 | tf_op jit(solution)/shard_map/ppermute | solution.py:308
  39.1 0.0 collective-permute-start.15
  39.1 2.0 %collective-permute-done.13.m_out = f32[9,16,128]{2,1,0:T(8,128)S(1)} collective-permute-done((f32[9,16,128]{2,1,0:T(8,128)S(1)}, f32[9,16,128]{2,1,0:T(8,128)S(1)}, u32[]{:S(2)}, u32[]{:S(2)}) %collective-permute-start.13) | collective-permute-done | bytes 73760 | tf_op jit(solution)/shard_map/ppermute | solution.py:311
  41.1 0.1 shard_map.86.m_out.m_mid
  41.2 0.0 collective-permute-done.12.m_in
  41.3 0.2 shard_map.87
  41.4 0.1 collective-permute-start.14
  41.5 0.0 collective-permute-done.10.f_out
  41.5 0.7 %shard_map.84 = f32[27,16,128]{2,1,0:T(8,128)} custom-call(f32[9,16,128]{2,1,0:T(8,128)S(1)} %get-tuple-element.43.f_in, f32[9,16,128]{2,1,0:T(8,128)S(1)} %get-tuple-element.44.f_mid, f32[9,16,128]{2,1,0:T(8,128)S(1)} %collective-permute-done.10.f_out), custom_call_target="tpu_custom_call" | custom-call | flops 200000 | bytes 1000000 | tf_op jit(solution)/shard_map/pallas_call | solution.py:291
  42.2 4.9 %collective-permute-done.15.m_out = f32[9,16,128]{2,1,0:T(8,128)S(1)} collective-permute-done((f32[9,16,128]{2,1,0:T(8,128)S(1)}, f32[9,16,128]{2,1,0:T(8,128)S(1)}, u32[]{:S(2)}, u32[]{:S(2)}) %collective-permute-start.15) | collective-permute-done | bytes 73760 | tf_op jit(solution)/shard_map/ppermute | solution.py:311
  47.1 0.1 shard_map.88.m_out
  47.2 0.0 collective-permute-done.14.m_in
  47.2 0.8 %shard_map.89 = (f32[27,16,128]{2,1,0:T(8,128)}, f32[3,16,128]{2,1,0:T(8,128)}) custom-call(f32[9,16,128]{2,1,0:T(8,128)S(1)} %collective-permute-done.14.m_in, f32[18,16,128]{2,1,0:T(8,128)S(1)} %get-tuple-element.57.m_mid, f32[18,16,128]{2,1,0:T(8,128)S(1)} %shard_map.88.m_out, f32[4,16,128]{2,1,0:T(8,128)S(1)} %get-tuple-element.59.saved, ...), custom_call_target="tpu_custom_call" | custom-call | flops 800000 | bytes 1000000 | tf_op jit(solution)/shard_map/pallas_call | solution.py:291
Async XLA Ops:
  0.6 0.7 %copy-start = (s32[1,2048]{1,0:T(1,128)S(1)}, s32[1,2048]{1,0:T(1,128)}, u32[]{:S(2)}) copy-start(s32[1,2048]{1,0:T(1,128)} %param.7) | copy-start | bytes 24580
  1.3 0.7 %copy-start.2 = (f32[3,1,2048]{2,1,0:T(1,128)S(1)}, f32[3,1,2048]{2,1,0:T(1,128)}, u32[]{:S(2)}) copy-start(f32[3,1,2048]{2,1,0:T(1,128)} %param.6) | copy-start | bytes 73732
  2.1 0.9 %copy-start.4 = (f32[27,1,2048]{2,1,0:T(1,128)S(1)}, f32[27,1,2048]{2,1,0:T(1,128)}, u32[]{:S(2)}) copy-start(f32[27,1,2048]{2,1,0:T(1,128)} %param.5) | copy-start | bytes 663556
  3.0 0.7 %copy-start.6 = (s32[1,2048]{1,0:T(1,128)S(1)}, s32[1,2048]{1,0:T(1,128)}, u32[]{:S(2)}) copy-start(s32[1,2048]{1,0:T(1,128)} %param.8) | copy-start | bytes 24580
  4.3 10.4 %collective-permute-start.1 = (f32[23,16,128]{2,1,0:T(8,128)S(1)}, f32[23,16,128]{2,1,0:T(8,128)S(1)}, u32[]{:S(2)}, u32[]{:S(2)}) collective-permute-start(f32[23,16,128]{2,1,0:T(8,128)S(1)} %get-tuple-element.34.f_out.f_mid), channel_id=1, source_target_pairs={{0,31},{1,2},{2,1},{3,4},{4,3},{5,6},{6,5},{7,8},{8,7},{9,10},{10,... | collective-permute-start | bytes 565256 | tf_op jit(solution)/shard_map/ppermute | solution.py:314
  10.8 1.3 %collective-permute-start.2 = (f32[9,16,128]{2,1,0:T(8,128)S(1)}, f32[9,16,128]{2,1,0:T(8,128)S(1)}, u32[]{:S(2)}, u32[]{:S(2)}) collective-permute-start(f32[9,16,128]{2,1,0:T(8,128)S(1)} %get-tuple-element.33), channel_id=1, source_target_pairs={{0,1},{1,0},{2,3},{3,2},{4,5},{5,4},{6,7},{7,6},{8,9},{9,8},{10,11... | collective-permute-start | bytes 221192 | tf_op jit(solution)/shard_map/ppermute | solution.py:308
  10.8 7.9 %collective-permute-start = (f32[9,16,128]{2,1,0:T(8,128)S(1)}, f32[9,16,128]{2,1,0:T(8,128)S(1)}, u32[]{:S(2)}, u32[]{:S(2)}) collective-permute-start(f32[9,16,128]{2,1,0:T(8,128)S(1)} %get-tuple-element.33), channel_id=1, source_target_pairs={{0,2},{1,31},{2,4},{3,1},{4,6},{5,3},{6,8},{7,5},{8,10},{9,7},{10,... | collective-permute-start | bytes 221192 | tf_op jit(solution)/shard_map/ppermute | solution.py:311
  15.3 4.0 %copy-start.5 = (f32[27,1,2048]{2,1,0:T(1,128)S(1)}, f32[27,1,2048]{2,1,0:T(1,128)}, u32[]{:S(2)}) copy-start(f32[27,1,2048]{2,1,0:T(1,128)} %param.9) | copy-start | bytes 663556
  15.3 9.7 %collective-permute-start.3 = (f32[9,16,128]{2,1,0:T(8,128)S(1)}, f32[9,16,128]{2,1,0:T(8,128)S(1)}, u32[]{:S(2)}, u32[]{:S(2)}) collective-permute-start(f32[9,16,128]{2,1,0:T(8,128)S(1)} %get-tuple-element.37), channel_id=1, source_target_pairs={{0,1},{1,0},{2,3},{3,2},{4,5},{5,4},{6,7},{7,6},{8,9},{9,8},{10,11... | collective-permute-start | bytes 221192 | tf_op jit(solution)/shard_map/ppermute | solution.py:308
  19.3 5.7 %copy-start.1 = (s32[1,2048]{1,0:T(1,128)S(1)}, s32[1,2048]{1,0:T(1,128)}, u32[]{:S(2)}) copy-start(s32[1,2048]{1,0:T(1,128)} %param.7) | copy-start | bytes 24580
  19.3 5.7 %copy-start.3 = (f32[3,1,2048]{2,1,0:T(1,128)S(1)}, f32[3,1,2048]{2,1,0:T(1,128)}, u32[]{:S(2)}) copy-start(f32[3,1,2048]{2,1,0:T(1,128)} %param.6) | copy-start | bytes 73732
  19.3 5.7 %copy-start.7 = (s32[1,2048]{1,0:T(1,128)S(1)}, s32[1,2048]{1,0:T(1,128)}, u32[]{:S(2)}) copy-start(s32[1,2048]{1,0:T(1,128)} %param.8) | copy-start | bytes 24580
  19.5 10.9 %collective-permute-start.6 = (f32[18,16,128]{2,1,0:T(8,128)S(1)}, f32[18,16,128]{2,1,0:T(8,128)S(1)}, u32[]{:S(2)}, u32[]{:S(2)}) collective-permute-start(f32[18,16,128]{2,1,0:T(8,128)S(1)} %get-tuple-element.41.m_in.m_mid), channel_id=1, source_target_pairs={{0,31},{1,2},{2,1},{3,4},{4,3},{5,6},{6,5},{7,8},{8,7},{9,10},{10,... | collective-permute-start | bytes 442376 | tf_op jit(solution)/shard_map/ppermute | solution.py:314
  21.9 7.9 %collective-permute-start.5 = (f32[9,16,128]{2,1,0:T(8,128)S(1)}, f32[9,16,128]{2,1,0:T(8,128)S(1)}, u32[]{:S(2)}, u32[]{:S(2)}) collective-permute-start(f32[9,16,128]{2,1,0:T(8,128)S(1)} %get-tuple-element.37), channel_id=1, source_target_pairs={{0,2},{1,31},{2,4},{3,1},{4,6},{5,3},{6,8},{7,5},{8,10},{9,7},{10,... | collective-permute-start | bytes 221192 | tf_op jit(solution)/shard_map/ppermute | solution.py:311
  21.9 8.5 %collective-permute-start.9 = (f32[9,16,128]{2,1,0:T(8,128)S(1)}, f32[9,16,128]{2,1,0:T(8,128)S(1)}, u32[]{:S(2)}, u32[]{:S(2)}) collective-permute-start(f32[9,16,128]{2,1,0:T(8,128)S(1)} %get-tuple-element.42), channel_id=1, source_target_pairs={{0,1},{1,0},{2,3},{3,2},{4,5},{5,4},{6,7},{7,6},{8,9},{9,8},{10,11... | collective-permute-start | bytes 221192 | tf_op jit(solution)/shard_map/ppermute | solution.py:308
  25.6 4.8 %collective-permute-start.8 = (f32[9,16,128]{2,1,0:T(8,128)S(1)}, f32[9,16,128]{2,1,0:T(8,128)S(1)}, u32[]{:S(2)}, u32[]{:S(2)}) collective-permute-start(f32[9,16,128]{2,1,0:T(8,128)S(1)} %get-tuple-element.38), channel_id=1, source_target_pairs={{0,1},{1,0},{2,3},{3,2},{4,5},{5,4},{6,7},{7,6},{8,9},{9,8},{10,11... | collective-permute-start | bytes 221192 | tf_op jit(solution)/shard_map/ppermute | solution.py:308
  25.7 8.1 %collective-permute-start.7 = (f32[9,16,128]{2,1,0:T(8,128)S(1)}, f32[9,16,128]{2,1,0:T(8,128)S(1)}, u32[]{:S(2)}, u32[]{:S(2)}) collective-permute-start(f32[9,16,128]{2,1,0:T(8,128)S(1)} %get-tuple-element.42), channel_id=1, source_target_pairs={{0,2},{1,31},{2,4},{3,1},{4,6},{5,3},{6,8},{7,5},{8,10},{9,7},{10,... | collective-permute-start | bytes 221192 | tf_op jit(solution)/shard_map/ppermute | solution.py:311
  29.8 7.9 %collective-permute-start.4 = (f32[9,16,128]{2,1,0:T(8,128)S(1)}, f32[9,16,128]{2,1,0:T(8,128)S(1)}, u32[]{:S(2)}, u32[]{:S(2)}) collective-permute-start(f32[9,16,128]{2,1,0:T(8,128)S(1)} %get-tuple-element.38), channel_id=1, source_target_pairs={{0,2},{1,31},{2,4},{3,1},{4,6},{5,3},{6,8},{7,5},{8,10},{9,7},{10,... | collective-permute-start | bytes 221192 | tf_op jit(solution)/shard_map/ppermute | solution.py:311
  31.0 7.3 %collective-permute-start.11 = (f32[9,16,128]{2,1,0:T(8,128)S(1)}, f32[9,16,128]{2,1,0:T(8,128)S(1)}, u32[]{:S(2)}, u32[]{:S(2)}) collective-permute-start(f32[9,16,128]{2,1,0:T(8,128)S(1)} %get-tuple-element.46), channel_id=1, source_target_pairs={{0,1},{1,0},{2,3},{3,2},{4,5},{5,4},{6,7},{7,6},{8,9},{9,8},{10,11... | collective-permute-start | bytes 221192 | tf_op jit(solution)/shard_map/ppermute | solution.py:308
  33.2 7.9 %collective-permute-start.13 = (f32[9,16,128]{2,1,0:T(8,128)S(1)}, f32[9,16,128]{2,1,0:T(8,128)S(1)}, u32[]{:S(2)}, u32[]{:S(2)}) collective-permute-start(f32[9,16,128]{2,1,0:T(8,128)S(1)} %get-tuple-element.46), channel_id=1, source_target_pairs={{0,2},{1,31},{2,4},{3,1},{4,6},{5,3},{6,8},{7,5},{8,10},{9,7},{10,... | collective-permute-start | bytes 221192 | tf_op jit(solution)/shard_map/ppermute | solution.py:311
  38.5 2.7 %collective-permute-start.12 = (f32[9,16,128]{2,1,0:T(8,128)S(1)}, f32[9,16,128]{2,1,0:T(8,128)S(1)}, u32[]{:S(2)}, u32[]{:S(2)}) collective-permute-start(f32[9,16,128]{2,1,0:T(8,128)S(1)} %get-tuple-element.51), channel_id=1, source_target_pairs={{0,1},{1,0},{2,3},{3,2},{4,5},{5,4},{6,7},{7,6},{8,9},{9,8},{10,11... | collective-permute-start | bytes 221192 | tf_op jit(solution)/shard_map/ppermute | solution.py:308
  38.6 2.9 %collective-permute-start.10 = (f32[9,16,128]{2,1,0:T(8,128)S(1)}, f32[9,16,128]{2,1,0:T(8,128)S(1)}, u32[]{:S(2)}, u32[]{:S(2)}) collective-permute-start(f32[9,16,128]{2,1,0:T(8,128)S(1)} %get-tuple-element.45), channel_id=1, source_target_pairs={{0,1},{1,0},{2,3},{3,2},{4,5},{5,4},{6,7},{7,6},{8,9},{9,8},{10,11... | collective-permute-start | bytes 221192 | tf_op jit(solution)/shard_map/ppermute | solution.py:308
  39.1 7.9 %collective-permute-start.15 = (f32[9,16,128]{2,1,0:T(8,128)S(1)}, f32[9,16,128]{2,1,0:T(8,128)S(1)}, u32[]{:S(2)}, u32[]{:S(2)}) collective-permute-start(f32[9,16,128]{2,1,0:T(8,128)S(1)} %get-tuple-element.51), channel_id=1, source_target_pairs={{0,2},{1,31},{2,4},{3,1},{4,6},{5,3},{6,8},{7,5},{8,10},{9,7},{10,... | collective-permute-start | bytes 221192 | tf_op jit(solution)/shard_map/ppermute | solution.py:311
  41.4 5.8 %collective-permute-start.14 = (f32[9,16,128]{2,1,0:T(8,128)S(1)}, f32[9,16,128]{2,1,0:T(8,128)S(1)}, u32[]{:S(2)}, u32[]{:S(2)}) collective-permute-start(f32[9,16,128]{2,1,0:T(8,128)S(1)} %get-tuple-element.56), channel_id=1, source_target_pairs={{0,1},{1,0},{2,3},{3,2},{4,5},{5,4},{6,7},{7,6},{8,9},{9,8},{10,11... | collective-permute-start | bytes 221192 | tf_op jit(solution)/shard_map/ppermute | solution.py:308
